TPU v7x, 32 devices: a whole 2x2x4 slice. The times are simulated.
32 devices in a mesh: section: 8 (over y, x, core), ctx: 4 (over z).
Axes of the slice: x: 2, y: 2, z: 4, core: 2. Of those that a mesh axis runs over, the one named last changes fastest.
Arguments:
- section_inputs: bfloat16 [8, 448, 2048], P('section', 'ctx'), may hold values from -3 to 3
- saved_inputs: bfloat16 [8, 448, 2048], P('section', 'ctx'), may hold values from -3 to 3
- output_grads: bfloat16 [8, 448, 2048], P('section', 'ctx'), may hold values from -6 to 6
- token_positions: int32 [448], P('ctx'), may hold values from 0 to 447, each once
- norm_gain: float32 [8, 2048], P('section'), may hold values from 0.7 to 6
- query_weight: bfloat16 [8, 2048, 2048], P('section', 'ctx'), may hold values from -0.13258252 to 0.13258252
- keyval_weight: bfloat16 [8, 2048, 1024], P('section', 'ctx'), may hold values from -0.13258252 to 0.13258252
- output_weight: bfloat16 [8, 2048, 2048], P('section'), may hold values from -0.125 to 0.125
Outputs:
- next_inputs: bfloat16 [8, 448, 2048], P('section', 'ctx')
- input_grads: bfloat16 [8, 448, 2048], P('section', 'ctx')
Inputs may be any that keep to these rules, and one draw needn't show every extreme that they name: `token_positions`: each position of the sequence once.
All inputs are finite; a program needn't handle non-finite values.
Results may differ from a plain program's by a relative error of at most 0.04.
The roundings to bfloat16 on the way count: a program that leaves them out, or rounds other values in their place, can miss the bound.
Values may be sent and summed in bfloat16 or wider, within the bound.
A program may use at most 192 MiB of HBM per device.

v0:
```python
import jax
import jax.numpy as jnp
from jax import lax
from jax.sharding import PartitionSpec as P

HEAD_DIM = 128


norm_eps = 1e-05
rope_base = 500000.0


def from_behind(block, axis, distance):
    devices = range(lax.axis_size(axis))
    route = [((i - distance) % len(devices), i) for i in devices]
    return lax.ppermute(block, axis, route)


def rotate(matrix, positions):
    half_dim = matrix.shape[-1] // 2
    frequency = rope_base ** (-2.0 * jnp.arange(half_dim, dtype=jnp.float32) / matrix.shape[-1])
    angles = positions.astype(jnp.float32)[:, None] * frequency[None, :]
    cos_table = jnp.cos(angles)[:, None, :]
    sin_table = jnp.sin(angles)[:, None, :]
    leading = matrix[..., :half_dim]
    trailing = matrix[..., half_dim:]
    return jnp.concatenate(
        [leading * cos_table - trailing * sin_table, trailing * cos_table + leading * sin_table],
        axis=-1,
    )


def project(tokens, gain, query_matrix, keyval_matrix, positions):
    widened = tokens.astype(jnp.float32)
    inverse = lax.rsqrt(jnp.mean(widened * widened, axis=-1, keepdims=True) + norm_eps)
    normed = (widened * inverse * gain[None, :]).astype(jnp.bfloat16)
    row_count = tokens.shape[0]
    query_full = jnp.dot(normed, query_matrix, preferred_element_type=jnp.float32)
    keyval_full = jnp.dot(normed, keyval_matrix, preferred_element_type=jnp.float32)
    queries = rotate(query_full.reshape(row_count, -1, HEAD_DIM), positions).astype(jnp.bfloat16)
    paired = keyval_full.reshape(row_count, 2, -1, HEAD_DIM)
    key_rows = rotate(paired[:, 0], positions).astype(jnp.bfloat16)
    value_rows = paired[:, 1].astype(jnp.bfloat16)
    return (queries, key_rows, value_rows)


def attend(queries, key_wide, value_wide, query_pos, key_pos, narrow):
    row_count = queries.shape[0]
    kv_count = key_wide.shape[1]
    head_size = queries.shape[2]
    group_size = queries.shape[1] // kv_count
    grouped = jnp.moveaxis(queries.reshape(row_count, kv_count, group_size, head_size), 1, 0)
    key_heads = jnp.moveaxis(key_wide, 1, 0)
    value_heads = jnp.moveaxis(value_wide, 1, 0)
    visible = (key_pos[None, :] <= query_pos[:, None])[None]

    def one_head(block):
        query_block, key_block, value_block = block
        scores = jnp.einsum(
            "rgd,sd->grs", query_block, key_block, preferred_element_type=jnp.float32
        ) * head_size ** (-0.5)
        masked = jnp.where(visible, scores, -1e30)
        row_max = lax.stop_gradient(jnp.max(masked, axis=-1, keepdims=True))
        numerators = jnp.where(visible, jnp.exp(masked - row_max), 0.0)
        totals = jnp.sum(numerators, axis=-1)
        if narrow:
            rounded = numerators.astype(jnp.bfloat16)
        else:
            rounded = lax.optimization_barrier(numerators.astype(jnp.bfloat16)).astype(jnp.float32)
        summed = jnp.einsum("grs,sd->rgd", rounded, value_block, preferred_element_type=jnp.float32)
        return summed / jnp.transpose(totals, (1, 0))[..., None]

    averaged = lax.map(one_head, (grouped, key_heads, value_heads))
    return jnp.moveaxis(averaged, 0, 1).reshape(row_count, -1).astype(jnp.bfloat16)


def finish(tokens, mixed, output_matrix):
    return (
        tokens.astype(jnp.float32)
        + jnp.dot(mixed, output_matrix, preferred_element_type=jnp.float32)
    ).astype(jnp.bfloat16)


def shards(
    section_inputs,
    saved_inputs,
    output_grads,
    token_positions,
    norm_gain,
    query_weight,
    keyval_weight,
    output_weight,
):
    key_positions = lax.all_gather(token_positions, "ctx", axis=0, tiled=True)
    full_query, full_keyval = (
        lax.all_gather(query_weight[0], "ctx", axis=0, tiled=True),
        lax.all_gather(keyval_weight[0], "ctx", axis=0, tiled=True),
    )
    full_output = output_weight[0]
    gain = norm_gain[0]
    forward_tokens = section_inputs[0]
    saved_tokens = saved_inputs[0]
    upstream = output_grads[0]

    def projector(tokens):
        return project(tokens, gain, full_query, full_keyval, token_positions)

    def attention_wide(queries, key_wide, value_wide):
        return attend(queries, key_wide, value_wide, token_positions, key_positions, False)

    def finishing(tokens, mixed):
        return finish(tokens, mixed, full_output)

    forward_queries, forward_keys, forward_values = projector(forward_tokens)
    (backward_queries, backward_keys, backward_values), back_project = jax.vjp(
        projector, saved_tokens
    )
    forward_keyset, forward_valueset = (
        lax.all_gather(forward_keys, "ctx", axis=0, tiled=True),
        lax.all_gather(forward_values, "ctx", axis=0, tiled=True),
    )
    mixed = attend(
        forward_queries, forward_keyset, forward_valueset, token_positions, key_positions, True
    )
    produced = finishing(forward_tokens, mixed)
    sent_on = from_behind(produced[None], "section", 1)
    backward_keyset, backward_valueset = (
        lax.all_gather(backward_keys, "ctx", axis=0, tiled=True),
        lax.all_gather(backward_values, "ctx", axis=0, tiled=True),
    )
    mixed, back_attend = jax.vjp(
        attention_wide,
        backward_queries.astype(jnp.float32),
        backward_keyset.astype(jnp.float32),
        backward_valueset.astype(jnp.float32),
    )
    produced, back_finish = jax.vjp(finishing, saved_tokens, mixed)
    residual_grad, mixed_grad = back_finish(upstream)
    query_grad, key_partial, value_partial = back_attend(mixed_grad)
    key_grads = lax.psum_scatter(
        key_partial.astype(jnp.bfloat16), "ctx", scatter_dimension=0, tiled=True
    )
    value_grads = lax.psum_scatter(
        value_partial.astype(jnp.bfloat16), "ctx", scatter_dimension=0, tiled=True
    )
    (project_grad,) = back_project((query_grad.astype(jnp.bfloat16), key_grads, value_grads))
    sent_back = from_behind((residual_grad + project_grad)[None], "section", -1)
    return (sent_on, sent_back)


def solution(mesh):
    placed = (
        P("section", "ctx", None),
        P("section", "ctx", None),
        P("section", "ctx", None),
        P("ctx"),
        P("section", None),
        P("section", "ctx", None),
        P("section", "ctx", None),
        P("section", None, None),
    )
    return jax.shard_map(
        shards,
        mesh=mesh,
        in_specs=placed,
        out_specs=(P("section", "ctx", None), P("section", "ctx", None)),
        check_vma=False,
    )
```

profile of v0, /device:TPU:17, one launch (start us, length us, event | category | flops | bytes accessed | tf_op | source)
XLA Modules:
  0.0 448.5 jit_solution(13387523796641160525)
XLA Ops:
  9.4 1.2 dynamic-slice
  12.2 4.0 all-reduce.6
  17.3 7.0 %fusion.134 = f32[112,2048]{1,0:T(8,128)S(1)} fusion(bf16[1,2048,2048]{2,1,0:T(8,128)(2,1)} %param.21, bf16[1,112,2048]{2,1,0:T(8,128)(2,1)S(1)} %copy-done.9), kind=kOutput, calls=%fused_computation.113 | convolution fusion | flops 939982848 | bytes 9764864 | tf_op jit(solution)/shard_map/transpose(jvp())/dot_general | solution.py:80
  24.3 1.6 reshape.244
  25.9 2.4 copy.47
  29.1 60.7 %all-gather.7.cloned.1.call-done = bf16[1,2048,1024]{2,1,0:T(8,128)(2,1)} async-done(((bf16[1,512,1024]{2,1,0:T(8,128)(2,1)}), bf16[1,2048,1024]{2,1,0:T(8,128)(2,1)}) %all-gather.7.cloned.1.call-update) | async-done | bytes 4194320 | tf_op jit(solution)/shard_map/all_gather | solution.py:97
  89.7 6.5 %copy.25 = bf16[1024,2048]{1,0:T(8,128)(2,1)} copy(bf16[1024,2048]{0,1:T(8,128)(2,1)} %bitcast.470) | data formatting | bytes 8388608 | tf_op jit(solution)/shard_map/dot_general | solution.py:39
  96.2 3.9 fusion.167
  100.2 1.5 fusion.165
  102.0 20.8 %all_gather.26 = bf16[448,4,128]{2,0,1:T(8,128)(2,1)} all-gather(bf16[112,4,128]{2,0,1:T(8,128)(2,1)S(1)} %pad_maximum_fusion.1), channel_id=1, replica_groups=mesh['section'=8,'ctx'=4] {'ctx'}, dimensions={0}, use_global_device_ids=true | all-gather | bytes 573440 | tf_op jit(solution)/shard_map/all_gather | solution.py:128
  122.8 23.1 %all-gather.3 = bf16[448,1,4,128]{3,0,2,1:T(8,128)(2,1)S(1)} all-gather(bf16[112,1,4,128]{3,0,2,1:T(8,128)(2,1)S(1)} %slice.82), channel_id=5, replica_groups=mesh['section'=8,'ctx'=4] {'ctx'}, dimensions={0}, use_global_device_ids=true | all-gather | bytes 573440 | tf_op jit(solution)/shard_map/all_gather | solution.py:129
  146.8 107.0 %all-gather.9.cloned.1.call-done = bf16[1,2048,2048]{2,1,0:T(8,128)(2,1)} async-done(((bf16[1,512,2048]{2,1,0:T(8,128)(2,1)}), bf16[1,2048,2048]{2,1,0:T(8,128)(2,1)}) %all-gather.9.cloned.1.call-update) | async-done | bytes 8388624 | tf_op jit(solution)/shard_map/all_gather | solution.py:96
  253.8 12.2 %copy.26 = bf16[2048,2048]{1,0:T(8,128)(2,1)} copy(bf16[2048,2048]{0,1:T(8,128)(2,1)} %bitcast.469) | data formatting | bytes 16777216 | tf_op jit(solution)/shard_map/dot_general | solution.py:38
  266.0 6.2 %fusion.169 = f32[112,16,128]{2,0,1:T(8,128)S(1)} fusion(bf16[16,128,2048]{2,1,0:T(8,128)(2,1)} %bitcast.465, bf16[1,112,2048]{2,1,0:T(8,128)(2,1)S(1)} %copy-done.1, f32[112]{0:T(128)S(1)} %fusion.178, f32[2048]{0:T(1024)S(1)} %bitcast.487), kind=kOutput, calls=%fused_computation.155 | convolution fusion | flops 940441600 | bytes 9773504 | tf_op jit(solution)/shard_map/jvp()/dot_general | solution.py:38
  273.7 21.6 %while.56 = (s32[]{:T(128)}, f32[4,4,112,448]{2,3,1,0:T(8,128)}, bf16[4,4,112,448]{2,3,1,0:T(8,128)(2,1)}, f32[4,112,4,1]{1,3,2,0:T(1,128)S(1)}, f32[4,112,4,128...) while((s32[]{:T(128)}, f32[4,4,112,448]{2,3,1,0:T(8,128)}, ...), condition=%wide.region_9.10_spmd.clone.clone, body=%wide.region_6.9_spmd.clone.sunk.clone | while | flops 104166720 | bytes 6184313 | solution.py:73
  273.7 2.4 bitcast_dynamic-update-slice_fusion.3
  276.4 2.0 fusion.260
  279.2 2.4 bitcast_dynamic-update-slice_fusion.3
  281.8 2.0 fusion.260
  284.6 2.3 bitcast_dynamic-update-slice_fusion.3
  287.2 1.9 fusion.260
  290.0 2.4 bitcast_dynamic-update-slice_fusion.3
  292.6 1.9 fusion.260
  296.3 44.5 %while.57 = (s32[]{:T(128)}, bf16[4,112,4,128]{3,1,2,0:T(8,128)(2,1)S(1)}, bf16[4,448,128]{2,1,0:T(8,128)(2,1)}, bf16[4,448,128]{2,1,0:T(8,128)(2,1)S(1)}, f32[4...) while((s32[]{:T(128)}, ...), condition=%wide.region_12.13_spmd.clone.clone, body=%wide.region_10.12_spmd.clone.sunk.clone | while | flops 208216064 | bytes 12119253 | solution.py:73
  296.3 1.3 fusion.270
  297.6 1.5 fusion.273
  299.8 2.2 convolution_convert_fusion.3
  302.0 1.2 constant_dynamic-slice_fusion.5
  303.6 2.3 fusion.272
  305.8 1.5 fusion.271
  307.4 1.3 fusion.270
  308.7 1.5 fusion.273
  311.0 2.2 convolution_convert_fusion.3
  314.7 2.3 fusion.272
  317.0 1.5 fusion.271
  318.5 1.3 fusion.270
  319.8 1.5 fusion.273
  322.1 2.2 convolution_convert_fusion.3
  325.9 2.3 fusion.272
  328.1 1.5 fusion.271
  329.6 1.3 fusion.270
  330.9 1.5 fusion.273
  333.2 2.2 convolution_convert_fusion.3
  337.0 2.3 fusion.272
  339.2 1.5 fusion.271
  340.8 17.3 %all-gather.1 = bf16[448,1,4,128]{3,0,2,1:T(8,128)(2,1)} all-gather(bf16[112,1,4,128]{3,0,2,1:T(8,128)(2,1)S(1)} %slice.83), channel_id=3, replica_groups=mesh['section'=8,'ctx'=4] {'ctx'}, dimensions={0}, use_global_device_ids=true | all-gather | bytes 573440 | tf_op jit(solution)/shard_map/all_gather | solution.py:120
  359.2 6.3 %fusion.172 = f32[112,16,128]{2,0,1:T(8,128)S(1)} fusion(bf16[16,128,2048]{2,1,0:T(8,128)(2,1)} %bitcast.466, bf16[1,112,2048]{2,1,0:T(8,128)(2,1)S(1)} %copy-done.2, f32[2048]{0:T(1024)} %bitcast.483, f32[112]{0:T(128)} %copy-done.18), kind=kOutput, calls=%fused_computation.158 | convolution fusion | flops 940441600 | bytes 9773504 | tf_op jit(solution)/shard_map/dot_general | solution.py:38
  367.2 6.2 %fusion.128 = bf16[112,2048]{1,0:T(8,128)(2,1)S(1)} fusion(bf16[1,2048,2048]{2,1,0:T(8,128)(2,1)} %all-gather.9.cloned.1.call-done, f32[112,16,64]{2,0,1:T(8,128)S(1)} %get-tuple-element.665, f32[112,16,64]{2,0,1:T(8,128)S(1)} %get-tuple-element.664), kind=kOutput, calls=%fused_computation.111 | convolution fusion | flops 939982848 | bytes 9764864 | tf_op jit(solution)/shard_map/transpose(jvp())/dot_general | solution.py:38
  374.7 11.1 %reduce-scatter.3.cloned.1.call-done = bf16[112,4,128]{2,0,1:T(8,128)(2,1)} async-done(((bf16[448,4,128]{2,0,1:T(8,128)(2,1)}), bf16[112,4,128]{2,0,1:T(8,128)(2,1)}) %reduce-scatter.3.cloned.1.call-update) | async-done | bytes 114704 | tf_op jit(solution)/shard_map/reduce_scatter | solution.py:143
  387.2 11.8 %all_gather.24 = bf16[448,4,128]{2,0,1:T(8,128)(2,1)S(1)} all-gather(bf16[112,4,128]{2,0,1:T(8,128)(2,1)S(1)} %pad_maximum_fusion), channel_id=1, replica_groups=mesh['section'=8,'ctx'=4] {'ctx'}, dimensions={0}, use_global_device_ids=true | all-gather | bytes 573440 | tf_op jit(solution)/shard_map/all_gather | solution.py:119
  398.9 3.8 fusion.154
  402.8 13.8 %while.55 = (s32[]{:T(128)}, bf16[4,112,4,128]{3,1,2,0:T(8,128)(2,1)S(1)}, bf16[4,448,128]{2,1,0:T(8,128)(2,1)}, bf16[4,448,128]{2,1,0:T(8,128)(2,1)S(1)}, bf16[...) while((s32[]{:T(128)}, bf16[4,112,4,128]{3,1,2,0:T(8,128)(2,1)S(1)}, ...), condition=%wide.region_4.5_spmd.clone.clone, body=%wide.region_1.4_spmd.clone.sunk.clone | while | flops 156256576 | bytes 1091605 | solution.py:73
  403.0 1.5 fusion.254
  404.5 1.8 fusion.255
  406.4 1.5 fusion.254
  407.9 1.8 fusion.255
  409.9 1.5 fusion.254
  411.4 1.8 fusion.255
  413.4 1.5 fusion.254
  414.8 1.8 fusion.255
  417.2 4.8 %fusion.146 = bf16[1,112,2048]{2,1,0:T(8,128)(2,1)S(1)} fusion(bf16[112,2048]{1,0:T(8,128)(2,1)S(1)} %convert_element_type.161, bf16[1,2048,2048]{2,1,0:T(8,128)(2,1)} %param.21, bf16[1,112,2048]{2,1,0:T(8,128)(2,1)S(1)} %copy-done.2), kind=kOutput, calls=%fused_computation.117 | convolution fusion | flops 940212224 | bytes 9764864 | tf_op jit(solution)/shard_map/dot_general | solution.py:80
  422.0 6.5 %collective-permute-start = (bf16[1,112,2048]{2,1,0:T(8,128)(2,1)S(1)}, bf16[1,112,2048]{2,1,0:T(8,128)(2,1)S(1)}, u32[]{:S(2)}, u32[]{:S(2)}) collective-permute-start(bf16[1,112,2048]{2,1,0:T(8,128)(2,1)S(1)} %fusion.146), channel_id=1, source_target_pairs={{28,0},{0,4},{4,8},{8,12},{12,16},{16,20},{20,24},{24,28},{29,1},{... | collective-permute-start | bytes 1376264 | tf_op jit(solution)/shard_map/ppermute | solution.py:16
  428.8 8.1 %collective-permute-done = bf16[1,112,2048]{2,1,0:T(8,128)(2,1)S(1)} collective-permute-done((bf16[1,112,2048]{2,1,0:T(8,128)(2,1)S(1)}, bf16[1,112,2048]{2,1,0:T(8,128)(2,1)S(1)}, u32[]{:S(2)}, u32[]{:S(2)}) %collective-permute-start) | collective-permute-done | bytes 458784 | tf_op jit(solution)/shard_map/ppermute | solution.py:16
  437.0 3.5 collective-permute-done.1
  (147 shorter events, 28.9 us)
Async XLA Ops:
  7.2 10.1 %copy-start.9 = (bf16[1,112,2048]{2,1,0:T(8,128)(2,1)S(1)}, bf16[1,112,2048]{2,1,0:T(8,128)(2,1)}, u32[]{:S(2)}) copy-start(bf16[1,112,2048]{2,1,0:T(8,128)(2,1)} %param.16) | copy-start | bytes 1376260
  7.2 82.6 %all-gather.7.cloned.1.call-start = ((), (), s32[]{:S(2)}) async-start(), calls=%async_computation.4 | async-start | bytes 5242880 | tf_op jit(solution)/shard_map/all_gather | solution.py:97
  7.9 245.9 %all-gather.9.cloned.1.call-start = ((), (), s32[]{:S(2)}) async-start(), calls=%async_computation.5 | async-start | bytes 10485760 | tf_op jit(solution)/shard_map/all_gather | solution.py:96
  8.7 364.8 %reduce-scatter.5.cloned.1.call-start = ((), (), s32[]{:S(2)}) async-start(), calls=%async_computation.3 | async-start | bytes 573440 | tf_op jit(solution)/shard_map/reduce_scatter | solution.py:140
  16.2 0.8 copy-start.13
  17.2 7.1 %copy-start.3 = (bf16[4,112,4,128]{3,1,2,0:T(8,128)(2,1)}, bf16[4,112,4,128]{3,1,2,0:T(8,128)(2,1)S(1)}, u32[]{:S(2)}) copy-start(bf16[4,112,4,128]{3,1,2,0:T(8,128)(2,1)S(1)} %fusion.188) | copy-start | bytes 1376260
  17.2 11.1 %copy-start.1 = (bf16[1,112,2048]{2,1,0:T(8,128)(2,1)S(1)}, bf16[1,112,2048]{2,1,0:T(8,128)(2,1)}, u32[]{:S(2)}) copy-start(bf16[1,112,2048]{2,1,0:T(8,128)(2,1)} %param.15) | copy-start | bytes 1376260
  24.3 4.3 copy-start.2
  28.6 67.7 %copy-start.19 = (f32[112]{0:T(128)}, f32[112]{0:T(128)S(1)}, u32[]{:S(2)}) copy-start(f32[112]{0:T(128)S(1)} %fusion.153) | copy-start | bytes 1348
  28.8 237.3 %copy-start.16 = (f32[112]{0:T(128)}, f32[112]{0:T(128)S(1)}, u32[]{:S(2)}) copy-start(f32[112]{0:T(128)S(1)} %fusion.178) | copy-start | bytes 1348
  28.8 67.5 %copy-start.18 = (f32[112]{0:T(128)}, f32[112]{0:T(128)S(1)}, u32[]{:S(2)}) copy-start(f32[112]{0:T(128)S(1)} %add_rsqrt_fusion) | copy-start | bytes 1348
  89.7 6.5 %copy-start.12 = (f32[1,2048]{1,0:T(1,128)S(1)}, f32[1,2048]{1,0:T(1,128)}, u32[]{:S(2)}) copy-start(f32[1,2048]{1,0:T(1,128)} %param.18) | copy-start | bytes 24580
  96.2 4.0 copy-start
  100.1 46.6 %copy-start.11 = (f32[112,2,4,128]{3,0,2,1:T(8,128)}, f32[112,2,4,128]{3,0,2,1:T(8,128)S(1)}, u32[]{:S(2)}) copy-start(f32[112,2,4,128]{3,0,2,1:T(8,128)S(1)} %fusion.167) | copy-start | bytes 1376260
  273.7 22.5 %copy-start.5 = (bf16[4,112,4,128]{3,1,2,0:T(8,128)(2,1)S(1)}, bf16[4,112,4,128]{3,1,2,0:T(8,128)(2,1)}, u32[]{:S(2)}) copy-start(bf16[4,112,4,128]{3,1,2,0:T(8,128)(2,1)} %copy-done.3) | copy-start | bytes 1376260
  299.1 0.8 copy-start.6
  303.6 3.8 copy-start.7
  310.2 0.8 copy-start.6
  314.7 3.8 copy-start.7
  321.3 0.8 copy-start.6
  325.8 3.8 copy-start.7
  332.5 0.8 copy-start.6
  337.0 3.8 copy-start.7
  340.7 18.4 %copy-start.8 = (bf16[4,448,128]{2,1,0:T(8,128)(2,1)}, bf16[4,448,128]{2,1,0:T(8,128)(2,1)S(1)}, u32[]{:S(2)}) copy-start(bf16[4,448,128]{2,1,0:T(8,128)(2,1)S(1)} %get-tuple-element.475) | copy-start | bytes 1376260
  340.8 45.1 %reduce-scatter.3.cloned.1.call-start = ((), (), s32[]{:S(2)}) async-start(), calls=%async_computation.2 | async-start | bytes 573440 | tf_op jit(solution)/shard_map/reduce_scatter | solution.py:143
  386.8 16.0 %copy-start.20 = (f32[112]{0:T(128)S(1)}, f32[112]{0:T(128)}, u32[]{:S(2)}) copy-start(f32[112]{0:T(128)} %copy-done.19) | copy-start | bytes 1348
  386.8 16.0 %copy-start.4 = (bf16[4,112,4,128]{3,1,2,0:T(8,128)(2,1)S(1)}, bf16[4,112,4,128]{3,1,2,0:T(8,128)(2,1)}, u32[]{:S(2)}) copy-start(bf16[4,112,4,128]{3,1,2,0:T(8,128)(2,1)} %copy-done.3) | copy-start | bytes 1376260
  386.8 16.0 %copy-start.14 = (s32[448]{0:T(512)S(1)}, s32[448]{0:T(512)}, u32[]{:S(2)}) copy-start(s32[448]{0:T(512)} %copy-done.13) | copy-start | bytes 5380
  386.8 16.0 %copy-start.15 = (s32[112]{0:T(128)S(1)}, s32[112]{0:T(128)}, u32[]{:S(2)}) copy-start(s32[112]{0:T(128)} %param.17) | copy-start | bytes 1348
  417.2 11.3 %copy-start.10 = (bf16[1,112,2048]{2,1,0:T(8,128)(2,1)S(1)}, bf16[1,112,2048]{2,1,0:T(8,128)(2,1)}, u32[]{:S(2)}) copy-start(bf16[1,112,2048]{2,1,0:T(8,128)(2,1)} %param.16) | copy-start | bytes 1376260
  417.2 11.3 %copy-start.17 = (f32[112]{0:T(128)S(1)}, f32[112]{0:T(128)}, u32[]{:S(2)}) copy-start(f32[112]{0:T(128)} %copy-done.16) | copy-start | bytes 1348
  422.0 15.0 %collective-permute-start = (bf16[1,112,2048]{2,1,0:T(8,128)(2,1)S(1)}, bf16[1,112,2048]{2,1,0:T(8,128)(2,1)S(1)}, u32[]{:S(2)}, u32[]{:S(2)}) collective-permute-start(bf16[1,112,2048]{2,1,0:T(8,128)(2,1)S(1)} %fusion.146), channel_id=1, source_target_pairs={{28,0},{0,4},{4,8},{8,12},{12,16},{16,20},{20,24},{24,28},{29,1},{... | collective-permute-start | bytes 1376264 | tf_op jit(solution)/shard_map/ppermute | solution.py:16
  428.8 11.7 %collective-permute-start.1 = (bf16[1,112,2048]{2,1,0:T(8,128)(2,1)S(1)}, bf16[1,112,2048]{2,1,0:T(8,128)(2,1)S(1)}, u32[]{:S(2)}, u32[]{:S(2)}) collective-permute-start(bf16[1,112,2048]{2,1,0:T(8,128)(2,1)S(1)} %fusion.164), channel_id=1, source_target_pairs={{4,0},{8,4},{12,8},{16,12},{20,16},{24,20},{28,24},{0,28},{5,1},{9... | collective-permute-start | bytes 1376264 | tf_op jit(solution)/shard_map/ppermute | solution.py:16
Sparse Core Ops, SparseCore 0:
  9.6 80.1 all-gather.6
  91.3 162.4 all-gather.8
  340.9 20.5 reduce-scatter.4
  365.6 20.1 reduce-scatter.2
where the time goes:
time: 453 us; the launch traced here: 449 us
  waiting for transfers between devices  192 us (42%)
  matrix products  99.9 us (22%)
  blocking collectives  77.1 us (17%)
  local copies, waits for them, and re-layouts  39.6 us (9%)
  other arithmetic  18.2 us (4%)
  between operations  14.9 us (3%)
  starting transfers between devices  6.69 us (1%)
    all_gather x1, waiting for transfers between devices, shards(): lax.all_gather(query_weight[0], 'ctx', axis=0, tiled=True)  107 us
    all_gather x1, waiting for transfers between devices, shards(): lax.all_gather(keyval_weight[0], 'ctx', axis=0, tiled=True)  60.7 us
    dot_general x16, matrix products, one_head(): jnp.einsum('grs,sd->rgd', rounded, value_block, preferred_element_type=jn...  29.8 us
    all_gather x1, blocking collectives, shards(): lax.all_gather(backward_values, 'ctx', axis=0, tiled=True)  23.1 us
    all_gather x1, blocking collectives, shards(): lax.all_gather(backward_keys, 'ctx', axis=0, tiled=True)  20.8 us
    dot_general x3, matrix products, project(): jnp.dot(normed, query_matrix, preferred_element_type=jnp.float32)  18.7 us
    all_gather x1, blocking collectives, shards(): lax.all_gather(forward_values, 'ctx', axis=0, tiled=True)  17.3 us
    sub x8, matrix products, one_head(): numerators = jnp.where(visible, jnp.exp(masked - row_max), 0.0)  15.4 us
  transfers between devices with their start and end apart: 6, of which 5 were waited for; matrix products, arithmetic and copies ran while one was open for 10% of the time, Pallas kernels for 0%

commit v1 on v0

--- a/solution.py
+++ b/solution.py
@@ -1,6 +1,10 @@
+import functools
+
 import jax
 import jax.numpy as jnp
 from jax import lax
+from jax.experimental import pallas as pl
+from jax.experimental.pallas import tpu as pltpu
 from jax.sharding import PartitionSpec as P
 
 HEAD_DIM = 128
@@ -148,6 +152,415 @@
     return (sent_on, sent_back)
 
 
+MESH = pl.DeviceIdType.MESH
+VMEM = pl.BlockSpec(memory_space=pltpu.VMEM)
+ANY = pl.BlockSpec(memory_space=pl.ANY)
+WIDE = jnp.float32
+SLIM = jnp.bfloat16
+
+
+def remote(src, dst, send, recv, device):
+    return pltpu.make_async_remote_copy(
+        src_ref=src, dst_ref=dst, send_sem=send, recv_sem=recv, device_id=device, device_id_type=MESH
+    )
+
+
+def sides(n, me, section):
+    for t in range(1, n):
+        for side, other, fits in ((0, me + t, me + t < n), (1, me - t, me - t >= 0)):
+            yield side, t, fits, other
+
+
+def gather_kernel(
+    n, nf, nb, up, wo_hbm, wq, wkv, pos, qkv_f, qkv_b, mg, wh, posg,
+    xf, xb, mgl, wo, xsend, xrecv, wsend, wrecv, msend, mrecv, psend, precv, own,
+):
+    section = lax.axis_index("section")
+    me = lax.axis_index("ctx")
+    depth, _ = wq.shape
+    gq = mg.shape[2]
+    wide = wh.shape[2]
+    kvw = (wide - gq) // 2
+    half = kvw * n
+
+    barrier = pltpu.get_barrier_semaphore()
+    for k in range(1, n):
+        pl.semaphore_signal(barrier, inc=1, device_id=(section, lax.rem(me + k, n)), device_id_type=MESH)
+    pl.semaphore_wait(barrier, n - 1)
+
+    def weight_copies(side, t, target, source):
+        parts = (
+            (wq, target * gq, gq, 0),
+            (wkv, target * kvw, kvw, gq),
+            (wkv, half + target * kvw, kvw, gq + kvw),
+        )
+        return [
+            remote(
+                ref.at[:, pl.ds(pl.multiple_of(start, 128), size)],
+                wh.at[source, :, pl.ds(to, size)],
+                wsend.at[side, t, i], wrecv.at[side, t, i], (section, target),
+            )
+            for i, (ref, start, size, to) in enumerate(parts)
+        ]
+
+    def row_copies(side, t, block, target):
+        pairs = ((nf, xf), (nb, xb))
+        return [
+            remote(
+                first if t == 1 else every.at[block], every.at[block],
+                xsend.at[side, t, i], xrecv.at[side, t, i], (section, target),
+            )
+            for i, (first, every) in enumerate(pairs)
+        ]
+
+    def small_copies(side, t, target):
+        return [remote(mgl.at[target], mg.at[me], msend.at[side, t], mrecv.at[side, t], (section, target))]
+
+    def place_copies(side, t, target):
+        return [remote(pos, posg.at[me], psend.at[side, t], precv.at[side, t], (section, target))]
+
+    def begin(copies):
+        for copy in copies:
+            copy.start()
+
+    def next_on(side):
+        return (me + 1, me + 1 < n) if side == 0 else (me - 1, me - 1 >= 0)
+
+    def behind(side, t):
+        return (me - t, me - t >= 0) if side == 0 else (me + t, me + t < n)
+
+    for side in (0, 1):
+        target, fits = next_on(side)
+        pl.when(fits)(lambda side=side, target=target: begin(row_copies(side, 1, me, target)))
+    for side, t, fits, other in sides(n, me, section):
+        pl.when(fits)(lambda side=side, t=t, other=other: begin(place_copies(side, t, other)))
+    wo_copy = pltpu.make_async_copy(wo_hbm, wo, own.at[0])
+    wo_copy.start()
+    mine = [
+        pltpu.make_async_copy(
+            ref.at[:, pl.ds(pl.multiple_of(start, 128), size)], wh.at[me, :, pl.ds(to, size)], own.at[i + 1]
+        )
+        for i, (ref, start, size, to) in enumerate(
+            ((wq, me * gq, gq, 0), (wkv, me * kvw, kvw, gq), (wkv, half + me * kvw, kvw, gq + kvw))
+        )
+    ]
+    begin(mine)
+    xf[me] = nf[...]
+    xb[me] = nb[...]
+    posg[me] = pos[...]
+
+    def send_weights(t):
+        for side, other, fits in ((0, me + t, me + t < n), (1, me - t, me - t >= 0)):
+            pl.when(fits)(
+                lambda side=side, other=other: begin(weight_copies(side, t, other, me))
+            )
+
+    send_weights(1)
+    wo_copy.wait()
+    for j in range(n):
+        mgl[j] = lax.dot_general(
+            up[...], wo[pl.ds(j * gq, gq), :], (((1,), (1,)), ((), ())), preferred_element_type=WIDE
+        ).astype(SLIM)
+    mg[me] = mgl[me]
+    for t in range(1, n):
+        if t > 1:
+            send_weights(t)
+        for side in (0, 1):
+            block, there = behind(side, t)
+            target, fits = next_on(side)
+
+            @pl.when(there)
+            def _():
+                for copy in row_copies(side, t, block, me):
+                    copy.wait_recv()
+
+            if t + 1 < n:
+                pl.when(jnp.logical_and(there, fits))(
+                    lambda side=side, target=target, block=block: begin(
+                        row_copies(side, t + 1, block, target)
+                    )
+                )
+    for side, t, fits, other in sides(n, me, section):
+        pl.when(fits)(lambda side=side, t=t, other=other: begin(small_copies(side, t, other)))
+
+    tile = 256 if wide % 256 == 0 else 128
+
+    def add_from(j, first):
+        columns = pl.ds(pl.multiple_of(j * depth, 128), depth)
+
+        @pl.loop(0, wide // tile)
+        def _(c):
+            at = pl.ds(pl.multiple_of(c * tile, 128), tile)
+            weights = wh[j, :, at]
+            for every, total in ((xf, qkv_f), (xb, qkv_b)):
+                rows = every[:, :, columns].reshape(-1, depth)
+                term = jnp.dot(rows, weights, preferred_element_type=WIDE)
+                total[:, at] = term if first else total[:, at] + term
+
+    for copy in mine:
+        copy.wait()
+    add_from(me, True)
+    for t in range(1, n):
+        for side in (0, 1):
+            block, there = behind(side, t)
+
+            @pl.when(there)
+            def _():
+                for copy in weight_copies(side, t, me, block):
+                    copy.wait_recv()
+                add_from(block, False)
+
+    for t in range(1, n):
+        for side in (0, 1):
+            block, there = behind(side, t)
+
+            @pl.when(there)
+            def _():
+                for copy in small_copies(side, t, me) + place_copies(side, t, me):
+                    copy.wait_recv()
+
+    for side, t, fits, other in sides(n, me, section):
+
+        @pl.when(fits)
+        def _():
+            for copy in (
+                weight_copies(side, t, other, me) + small_copies(side, t, other) + place_copies(side, t, other)
+            ):
+                copy.wait_send()
+
+    for t in range(1, n):
+        for side in (0, 1):
+            block, there = behind(side, t - 1)
+            target, fits = next_on(side)
+
+            @pl.when(jnp.logical_and(there, fits))
+            def _():
+                for copy in row_copies(side, t, block, target):
+                    copy.wait_send()
+
+
+def attend_kernel(qkv_f, qkv_b, mg, cos, sin, qpos, kpos, mixed, dqkv):
+    gq = mg.shape[1]
+    kvw = (qkv_f.shape[1] - gq) // 2
+    group = gq // kvw
+    scale = HEAD_DIM ** (-0.5)
+    visible = kpos[...] <= qpos[...]
+
+    def turn(block, sign):
+        return block * cos[...] + sign * (pltpu.roll(block, HEAD_DIM // 2, 1) * sin[...])
+
+    def dot(a, b, dims):
+        return lax.dot_general(a, b, (dims, ((), ())), preferred_element_type=WIDE)
+
+    def weigh(queries, keys):
+        scores = dot(queries, keys, ((1,), (1,))) * scale
+        masked = jnp.where(visible, scores, -1e30)
+        row_max = jnp.max(masked, axis=-1, keepdims=True)
+        numerators = jnp.where(visible, jnp.exp(masked - row_max), 0.0)
+        return numerators, jnp.sum(numerators, axis=-1, keepdims=True)
+
+    for kv in range(kvw // HEAD_DIM):
+        key_at = pl.ds(gq + kv * HEAD_DIM, HEAD_DIM)
+        value_at = pl.ds(gq + kvw + kv * HEAD_DIM, HEAD_DIM)
+        keys_f, values_f = turn(qkv_f[:, key_at], 1.0).astype(SLIM), qkv_f[:, value_at].astype(SLIM)
+        keys_b, values_b = turn(qkv_b[:, key_at], 1.0).astype(SLIM), qkv_b[:, value_at].astype(SLIM)
+
+        def head(h, grads):
+            at = pl.ds(pl.multiple_of((kv * group + h) * HEAD_DIM, HEAD_DIM), HEAD_DIM)
+            queries = turn(qkv_f[:, at], 1.0).astype(SLIM)
+            numerators, totals = weigh(queries, keys_f)
+            mixed[:, at] = (dot(numerators.astype(SLIM), values_f, ((1,), (0,))) / totals).astype(SLIM)
+
+            queries = turn(qkv_b[:, at], 1.0).astype(SLIM)
+            numerators, totals = weigh(queries, keys_b)
+            rounded = numerators.astype(SLIM)
+            summed = dot(rounded, values_b, ((1,), (0,)))
+            grad = mg[:, at].astype(WIDE)
+            summed_grad = grad / totals
+            totals_grad = -jnp.sum(summed_grad * (summed / totals), axis=-1, keepdims=True)
+            narrow_grad = summed_grad.astype(SLIM)
+            numer_grad = dot(narrow_grad, values_b, ((1,), (1,))) + totals_grad
+            score_grad = (numerators * numer_grad * scale).astype(SLIM)
+            query_grad = dot(score_grad, keys_b, ((1,), (0,))).astype(SLIM)
+            dqkv[:, at] = turn(query_grad.astype(WIDE), -1.0).astype(SLIM)
+            key_grad, value_grad = grads
+            return (
+                key_grad + dot(score_grad, queries, ((0,), (0,))),
+                value_grad + dot(rounded, narrow_grad, ((0,), (0,))),
+            )
+
+        nothing = jnp.zeros(keys_b.shape, WIDE)
+        key_grad, value_grad = lax.fori_loop(0, group, head, (nothing, nothing))
+        dqkv[:, key_at] = turn(key_grad.astype(SLIM).astype(WIDE), -1.0).astype(SLIM)
+        dqkv[:, value_at] = value_grad.astype(SLIM)
+
+
+def finish_kernel(
+    n, sections, mixed, dqkv, wh, wo_hbm, tokens, saved, upstream, gain, ahead, back,
+    mixed_in, part, part_in, wo, produced, grads, asend, arecv, bsend, brecv, csend, crecv, own,
+):
+    section = lax.axis_index("section")
+    me = lax.axis_index("ctx")
+    gq = mixed.shape[2]
+    depth = wh.shape[1]
+    following, preceding = lax.rem(section + 1, sections), lax.rem(section + sections - 1, sections)
+
+    barrier = pltpu.get_barrier_semaphore()
+    for k in range(1, n):
+        pl.semaphore_signal(barrier, inc=1, device_id=(section, lax.rem(me + k, n)), device_id_type=MESH)
+    for other in (following, preceding):
+        pl.semaphore_signal(barrier, inc=1, device_id=(other, me), device_id_type=MESH)
+    pl.semaphore_wait(barrier, n + 1)
+
+    wo_copy = pltpu.make_async_copy(wo_hbm, wo, own)
+    wo_copy.start()
+
+    def mixed_copy(k, target):
+        return remote(mixed.at[target], mixed_in.at[k], asend.at[k], arecv.at[k], (section, target))
+
+    def part_copy(k, target):
+        return remote(part.at[k], part_in.at[k], bsend.at[k], brecv.at[k], (section, target))
+
+    order = [n // 2] + [k for k in range(1, n) if k != n // 2]
+    for k in order:
+        mixed_copy(k, lax.rem(me + k, n)).start()
+
+    def partial_grad(target, k):
+        rows = dqkv[target]
+        for j in range(n):
+            part[k, :, pl.ds(j * depth, depth)] = lax.dot_general(
+                rows, wh[j], (((1,), (1,)), ((), ())), preferred_element_type=WIDE
+            ).astype(SLIM)
+
+    for k in order:
+        target = lax.rem(me + k, n)
+        partial_grad(target, k)
+        part_copy(k, target).start()
+    partial_grad(me, 0)
+    wo_copy.wait()
+
+    def from_source(k):
+        return lax.rem(me + n - k, n)
+
+    total = tokens[...].astype(WIDE)
+    total += jnp.dot(
+        mixed[me], wo[pl.ds(pl.multiple_of(me * gq, 128), gq), :], preferred_element_type=WIDE
+    )
+    for k in range(1, n):
+        mixed_copy(k, me).wait_recv()
+        rows = pl.ds(pl.multiple_of(from_source(k) * gq, 128), gq)
+        total += jnp.dot(mixed_in[k], wo[rows, :], preferred_element_type=WIDE)
+    produced[...] = total.astype(SLIM)
+
+    ahead_copy = remote(produced, ahead, csend.at[0], crecv.at[0], (following, me))
+    ahead_copy.start()
+
+    widened = saved[...].astype(WIDE)
+    inverse = lax.rsqrt(jnp.mean(widened * widened, axis=-1, keepdims=True) + norm_eps)
+    normed_grad = part[0].astype(WIDE)
+    for k in range(1, n):
+        part_copy(k, me).wait_recv()
+        normed_grad += part_in[k].astype(WIDE)
+    scaled = normed_grad.astype(SLIM).astype(WIDE) * gain[...]
+    inner = jnp.mean(scaled * widened, axis=-1, keepdims=True)
+    project_grad = inverse * scaled - widened * (inverse * inverse * inverse * inner)
+    grads[...] = upstream[...] + project_grad.astype(SLIM)
+
+    back_copy = remote(grads, back, csend.at[1], crecv.at[1], (preceding, me))
+    back_copy.start()
+    for k in range(1, n):
+        mixed_copy(k, lax.rem(me + k, n)).wait_send()
+        part_copy(k, lax.rem(me + k, n)).wait_send()
+    ahead_copy.wait()
+    back_copy.wait()
+
+
+def by_heads(n, sections):
+    def step(
+        section_inputs, saved_inputs, output_grads, token_positions, norm_gain,
+        query_weight, keyval_weight, output_weight,
+    ):
+        _, rows, width = section_inputs.shape
+        _, depth, query_width = query_weight.shape
+        gq = query_width // n
+        wide = gq + keyval_weight.shape[2] // n
+        limit = 60 * 2**20
+
+        def norm(tokens):
+            widened = tokens.astype(WIDE)
+            inverse = lax.rsqrt(jnp.mean(widened * widened, axis=-1, keepdims=True) + norm_eps)
+            return (widened * inverse * norm_gain).astype(SLIM)
+
+        def shaped(shape, kind=SLIM):
+            return jax.ShapeDtypeStruct(shape, kind)
+
+        dma = pltpu.SemaphoreType.DMA
+        qkv_f, qkv_b, mixed_grad, head_weights, places = pl.pallas_call(
+            functools.partial(gather_kernel, n),
+            out_shape=(
+                shaped((n * rows, wide), WIDE), shaped((n * rows, wide), WIDE), shaped((n, rows, gq)),
+                shaped((n, depth, wide)), shaped((n, 1, rows), jnp.int32),
+            ),
+            in_specs=[VMEM, VMEM, VMEM, ANY, ANY, ANY, VMEM],
+            out_specs=(VMEM,) * 5,
+            scratch_shapes=[
+                pltpu.VMEM((n, rows, width), SLIM), pltpu.VMEM((n, rows, width), SLIM),
+                pltpu.VMEM((n, rows, gq), SLIM), pltpu.VMEM((query_width, width), SLIM),
+                dma((2, n, 2)), dma((2, n, 2)), dma((2, n, 3)), dma((2, n, 3)),
+                dma((2, n)), dma((2, n)), dma((2, n)), dma((2, n)), dma((4,)),
+            ],
+            compiler_params=pltpu.CompilerParams(
+                collective_id=0, has_side_effects=True, vmem_limit_bytes=limit
+            ),
+            name="gather",
+        )(
+            norm(section_inputs[0]), norm(saved_inputs[0]), output_grads[0], output_weight[0],
+            query_weight[0], keyval_weight[0], token_positions[None],
+        )
+
+        positions = places.reshape(-1)
+        half_dim = HEAD_DIM // 2
+        frequency = rope_base ** (-2.0 * jnp.arange(half_dim, dtype=WIDE) / HEAD_DIM)
+        angles = positions.astype(WIDE)[:, None] * frequency[None, :]
+        cos_table, sin_table = jnp.cos(angles), jnp.sin(angles)
+        cos_table = jnp.concatenate([cos_table, cos_table], axis=-1)
+        sin_table = jnp.concatenate([-sin_table, sin_table], axis=-1)
+        mixed, qkv_grad = pl.pallas_call(
+            attend_kernel,
+            out_shape=(shaped((n * rows, gq)), shaped((n * rows, wide))),
+            in_specs=[VMEM] * 7,
+            out_specs=(VMEM,) * 2,
+            compiler_params=pltpu.CompilerParams(vmem_limit_bytes=limit),
+            name="attend",
+        )(
+            qkv_f, qkv_b, mixed_grad.reshape(n * rows, gq), cos_table, sin_table,
+            positions[:, None], positions[None, :],
+        )
+
+        ahead, back = pl.pallas_call(
+            functools.partial(finish_kernel, n, sections),
+            out_shape=(shaped((rows, width)), shaped((rows, width))),
+            in_specs=[VMEM, VMEM, VMEM, ANY, VMEM, VMEM, VMEM, VMEM],
+            out_specs=(VMEM,) * 2,
+            scratch_shapes=[
+                pltpu.VMEM((n, rows, gq), SLIM), pltpu.VMEM((n, rows, width), SLIM),
+                pltpu.VMEM((n, rows, width), SLIM), pltpu.VMEM((query_width, width), SLIM),
+                pltpu.VMEM((rows, width), SLIM), pltpu.VMEM((rows, width), SLIM),
+                dma((n,)), dma((n,)), dma((n,)), dma((n,)), dma((2,)), dma((2,)), dma,
+            ],
+            compiler_params=pltpu.CompilerParams(
+                collective_id=1, has_side_effects=True, vmem_limit_bytes=limit
+            ),
+            name="finish",
+        )(
+            mixed.reshape(n, rows, gq), qkv_grad.reshape(n, rows, wide), head_weights, output_weight[0],
+            section_inputs[0], saved_inputs[0], output_grads[0], norm_gain,
+        )
+        return (ahead[None], back[None])
+
+    return step
+
+
 def solution(mesh):
     placed = (
         P("section", "ctx", None),
@@ -159,8 +572,16 @@
         P("section", "ctx", None),
         P("section", None, None),
     )
+    n, sections = mesh.shape["ctx"], mesh.shape["section"]
+
+    def chosen(*blocks):
+        kv_heads = blocks[6].shape[2] // (2 * HEAD_DIM)
+        if n > 1 and sections > 2 and kv_heads % n == 0:
+            return by_heads(n, sections)(*blocks)
+        return shards(*blocks)
+
     return jax.shard_map(
-        shards,
+        chosen,
         mesh=mesh,
         in_specs=placed,
         out_specs=(P("section", "ctx", None), P("section", "ctx", None)),

time: 453 us -> 239 us (0.53)
  Pallas kernels: 0 us -> 222 us
  waiting for transfers between devices: 192 us -> 0 us
  matrix products: 99.9 us -> 0 us
  blocking collectives: 77.1 us -> 0 us
  local copies, waits for them, and re-layouts: 39.6 us -> 6.47 us
  between operations: 14.9 us -> 0.68 us
  other arithmetic: 18.2 us -> 9.34 us
  starting transfers between devices: 6.69 us -> 0 us
    pallas_call x0 -> x3, Pallas kernels: none -> 222 us  [the longest x1 142 us: step(): pl.pallas_call(functools.partial(gather_kernel, n), out_shape=(shaped((n...]
    all_gather x2 -> x0, waiting for transfers between devices: 168 us -> none  [the longest x1 107 us: shards(): lax.all_gather(query_weight[0], 'ctx', axis=0, tiled=True)]
    dot_general x32 -> x0, matrix products: 84.5 us -> none  [the longest x16 29.8 us: one_head(): jnp.einsum('grs,sd->rgd', rounded, value_block, preferred_element_type=jn...]
    all_gather x4 -> x0, blocking collectives: 73 us -> none  [the longest x1 23.1 us: shards(): lax.all_gather(backward_values, 'ctx', axis=0, tiled=True)]
    dot_general x2 -> x0, local copies, waits for them, and re-layouts: 18.7 us -> none  [the longest x1 12.2 us: project(): jnp.dot(normed, query_matrix, preferred_element_type=jnp.float32)]
    sub x8 -> x0, matrix products: 15.4 us -> none  [one_head(): numerators = jnp.where(visible, jnp.exp(masked - row_max), 0.0)]
    ppermute x2 -> x0, waiting for transfers between devices: 11.6 us -> none  [from_behind(): return lax.ppermute(block, axis, route)]
    reduce_scatter x2 -> x0, waiting for transfers between devices: 11.1 us -> none  [the longest x1 11.1 us: shards(): lax.psum_scatter(value_partial.astype(jnp.bfloat16), 'ctx', scatter_dimen...]
  transfers between devices with their start and end apart: 6 -> 0, of which waited for: 5 -> 0; matrix products, arithmetic and copies ran while one was open for 10% -> 0% of each run, Pallas kernels for 0% -> 0%
where the time goes in v1:
time: 239 us
  Pallas kernels  222 us (93%)
  other arithmetic  9.34 us (4%)
  local copies, waits for them, and re-layouts  6.47 us (3%)
    pallas_call x1, Pallas kernels, step(): pl.pallas_call(functools.partial(gather_kernel, n), out_shape=(shaped((n...  142 us
    pallas_call x1, Pallas kernels, step(): pl.pallas_call(functools.partial(finish_kernel, n, sections), out_shape=(...  68.2 us
    pallas_call x1, Pallas kernels, step(): pl.pallas_call(attend_kernel, out_shape=(shaped((n * rows, gq)), shaped((...  11.8 us

profile of v1, /device:TPU:17, one launch (start us, length us, event | category | flops | bytes accessed | tf_op | source)
XLA Modules:
  0.0 238.8 jit_solution(11078167833212869170)
XLA Ops:
  0.6 1.2 fusion
  1.8 1.2 fusion.3
  3.1 2.4 fusion.5
  5.5 142.3 %gather.1 = (f32[448,768]{1,0:T(8,128)}, f32[448,768]{1,0:T(8,128)}, bf16[4,112,512]{2,1,0:T(8,128)(2,1)}, bf16[4,512,768]{2,1,0:T(8,128)(2,1)}, s32[4,1,112]{2,1,0:T(1,128)}) custom-call(bf16[112,2048]{1,0:T(8,128)(2,1)} %get-tuple-element.21.nf, bf16[112,2048]{1,0:T(8,128)(2,1)} %get-tuple-element.20.nb, bf16[112,2048]{1,0:T(8,128)(2,1)} %bitcast.23, ...), custom_call_target="tpu_custom_call" | custom-call | tf_op jit(solution)/shard_map/gather/pallas_call | solution.py:498
  147.7 0.5 broadcast.53
  148.3 1.3 reduce.9
  149.6 1.3 broadcast_in_dim_reshape.4.kpos
  150.9 0.7 convert_reduce_fusion
  151.6 0.1 convert_element_type.27
  151.7 0.9 reshape.47.qpos
  152.6 0.9 fusion.6
  153.5 0.8 pad_maximum_fusion.1.sin
  154.3 0.8 pad_maximum_fusion.cos
  155.1 11.8 %attend.1 = (bf16[448,512]{1,0:T(8,128)(2,1)}, bf16[448,768]{1,0:T(8,128)(2,1)}) custom-call(f32[448,768]{1,0:T(8,128)} %get-tuple-element.11.qkv_f, f32[448,768]{1,0:T(8,128)} %get-tuple-element.12.qkv_b, bf16[448,512]{1,0:T(8,128)(2,1)} %bitcast.27, f32[448,128]{1,0:T(8,128)} %pad_maximum_fusion.cos, f32[448,128]{1,0:T(8,128)} %pad_maximum_fusion.1.sin, ...), custom_call_target="tpu_custom_call" | custom-call | tf_op jit(solution)/shard_map/attend/pallas_call | solution.py:528
  166.9 68.2 %finish.1 = (bf16[112,2048]{1,0:T(8,128)(2,1)}, bf16[112,2048]{1,0:T(8,128)(2,1)}) custom-call(bf16[4,112,512]{2,1,0:T(8,128)(2,1)} %bitcast.30, bf16[4,112,768]{2,1,0:T(8,128)(2,1)} %bitcast.26, bf16[4,512,768]{2,1,0:T(8,128)(2,1)} %get-tuple-element.17.wh, bf16[2048,2048]{1,0:T(8,128)(2,1)} %bitcast.19, bf16[112,2048]{1,0:T(8,128)(2,1)} %bitcast.21, ...), custom_call_target="tpu_custom_call" | custom-call | tf_op jit(solution)/shard_map/finish/pallas_call | solution.py:540
  235.2 1.8 copy.13
  237.0 1.8 copy.14
  (2 shorter events, 0.0 us)

commit v2 on v0

--- a/solution.py
+++ b/solution.py
@@ -1,6 +1,10 @@
+import functools
+
 import jax
 import jax.numpy as jnp
 from jax import lax
+from jax.experimental import pallas as pl
+from jax.experimental.pallas import tpu as pltpu
 from jax.sharding import PartitionSpec as P
 
 HEAD_DIM = 128
@@ -148,6 +152,413 @@
     return (sent_on, sent_back)
 
 
+MESH = pl.DeviceIdType.MESH
+VMEM = pl.BlockSpec(memory_space=pltpu.VMEM)
+ANY = pl.BlockSpec(memory_space=pl.ANY)
+WIDE = jnp.float32
+SLIM = jnp.bfloat16
+
+
+def remote(src, dst, send, recv, device):
+    return pltpu.make_async_remote_copy(
+        src_ref=src, dst_ref=dst, send_sem=send, recv_sem=recv, device_id=device, device_id_type=MESH
+    )
+
+
+def layer_kernel(
+    n, sections, nf, nb, up, wo_hbm, wq, wkv, pos, waves, tokens, saved, gain, ahead, back,
+    xf, xb, mgl, mg, wo, wh, posg, qcol, cos, sin, qkv_f, qkv_b, mixed, dqkv, mixed_in, part, inbox,
+    produced, grads, fsend, frecv, gsend, grecv, wsend, wrecv, msend, mrecv, psend, precv,
+    asend, arecv, bsend, brecv, csend, crecv, own,
+):
+    section = lax.axis_index("section")
+    me = lax.axis_index("ctx")
+    depth, _ = wq.shape
+    rows, gq = mg.shape[1:]
+    wide = wh.shape[2]
+    kvw = (wide - gq) // 2
+    half = kvw * n
+    group = gq // kvw
+    scale = HEAD_DIM ** (-0.5)
+    following, preceding = lax.rem(section + 1, sections), lax.rem(section + sections - 1, sections)
+
+    barrier = pltpu.get_barrier_semaphore()
+    for k in range(1, n):
+        pl.semaphore_signal(barrier, inc=1, device_id=(section, lax.rem(me + k, n)), device_id_type=MESH)
+    for other in (following, preceding):
+        pl.semaphore_signal(barrier, inc=1, device_id=(other, me), device_id_type=MESH)
+    pl.semaphore_wait(barrier, n + 1)
+
+    def peer(side, t):
+        return (me + t, me + t < n) if side == 0 else (me - t, me - t >= 0)
+
+    def behind(side, t):
+        return peer(1 - side, t)
+
+    def begin(copies):
+        for copy in copies:
+            copy.start()
+
+    def arrive(copies):
+        for copy in copies:
+            copy.wait_recv()
+
+    def leave(copies):
+        for copy in copies:
+            copy.wait_send()
+
+    def weight_copies(side, t, target, source):
+        parts = (
+            (wq, target * gq, gq, 0),
+            (wkv, target * kvw, kvw, gq),
+            (wkv, half + target * kvw, kvw, gq + kvw),
+        )
+        return [
+            remote(
+                ref.at[:, pl.ds(pl.multiple_of(start, 128), size)],
+                wh.at[source, :, pl.ds(to, size)],
+                wsend.at[side, t, i], wrecv.at[side, t, i], (section, target),
+            )
+            for i, (ref, start, size, to) in enumerate(parts)
+        ]
+
+    relays = ((nf, xf, fsend, frecv), (nb, xb, gsend, grecv))
+
+    def row_copies(batch, side, t, block, target):
+        first, every, send, recv = relays[batch]
+        return [
+            remote(
+                first if t == 1 else every.at[block], every.at[block],
+                send.at[side, t], recv.at[side, t], (section, target),
+            )
+        ]
+
+    def small_copies(side, t, target):
+        return [remote(mgl.at[target], mg.at[me], msend.at[side, t], mrecv.at[side, t], (section, target))]
+
+    def place_copies(side, t, target):
+        return [remote(pos, posg.at[me], psend.at[side, t], precv.at[side, t], (section, target))]
+
+    def mixed_copies(side, t, target):
+        return [
+            remote(mixed.at[target], mixed_in.at[me], asend.at[side, t], arecv.at[side, t], (section, target))
+        ]
+
+    def hop(batch, side, t):
+        block, there = behind(side, t)
+        target, fits = peer(side, 1)
+        pl.when(there)(lambda: arrive(row_copies(batch, side, t, block, me)))
+        if t + 1 < n:
+            pl.when(jnp.logical_and(there, fits))(
+                lambda: begin(row_copies(batch, side, t + 1, block, target))
+            )
+
+    def send_own(batch):
+        for side in (0, 1):
+            target, fits = peer(side, 1)
+            pl.when(fits)(lambda: begin(row_copies(batch, side, 1, me, target)))
+
+    def to_all(copies, action):
+        for t in range(n - 1, 0, -1):
+            for side in (0, 1):
+                target, fits = peer(side, t)
+                pl.when(fits)(lambda: action(copies(side, t, target)))
+
+    def from_all(copies):
+        for t in range(1, n):
+            for side in (0, 1):
+                _, there = behind(side, t)
+                pl.when(there)(lambda: arrive(copies(side, t, me)))
+
+    send_own(0)
+    to_all(place_copies, begin)
+    wo_copy = pltpu.make_async_copy(wo_hbm, wo, own.at[0])
+    wo_copy.start()
+    mine = [
+        pltpu.make_async_copy(
+            ref.at[:, pl.ds(pl.multiple_of(start, 128), size)], wh.at[me, :, pl.ds(to, size)], own.at[i + 1]
+        )
+        for i, (ref, start, size, to) in enumerate(
+            ((wq, me * gq, gq, 0), (wkv, me * kvw, kvw, gq), (wkv, half + me * kvw, kvw, gq + kvw))
+        )
+    ]
+    begin(mine)
+    posg[me] = pos[...]
+    xf[me] = nf[...]
+    xb[me] = nb[...]
+
+    def send_weights(side):
+        for t in range(n - 1, 0, -1):
+            target, fits = peer(side, t)
+            pl.when(fits)(lambda: begin(weight_copies(side, t, target, me)))
+
+    for t in range(1, n):
+        pl.when(me == t - 1)(lambda: send_weights(0))
+        pl.when(n - me == t)(lambda: send_weights(1))
+        for side in (0, 1):
+            hop(0, side, t)
+
+    wo_copy.wait()
+    for j in range(n):
+        mgl[j] = lax.dot_general(
+            up[...], wo[pl.ds(j * gq, gq), :], (((1,), (1,)), ((), ())), preferred_element_type=WIDE
+        ).astype(SLIM)
+    mg[me] = mgl[me]
+    send_own(1)
+    to_all(small_copies, begin)
+
+    from_all(place_copies)
+    for j in range(n):
+        column = jnp.transpose(jnp.broadcast_to(posg[j].astype(WIDE), (HEAD_DIM, rows)))
+        angles = column * waves[0:1, :]
+        qcol[j] = column
+        cos[pl.ds(j * rows, rows), :] = jnp.cos(angles)
+        sin[pl.ds(j * rows, rows), :] = jnp.sin(angles) * waves[1:2, :]
+
+    tile = 256 if wide % 256 == 0 else 128
+
+    def add_from(j, first):
+        columns = pl.ds(pl.multiple_of(j * depth, 128), depth)
+
+        @pl.loop(0, wide // tile)
+        def _(c):
+            at = pl.ds(pl.multiple_of(c * tile, 128), tile)
+            term = jnp.dot(
+                xf[:, :, columns].reshape(-1, depth), wh[j, :, at], preferred_element_type=WIDE
+            )
+            qkv_f[:, at] = term if first else qkv_f[:, at] + term
+
+    for copy in mine:
+        copy.wait()
+    add_from(me, True)
+    for t in range(1, n):
+        for side in (0, 1):
+            block, there = behind(side, t)
+
+            @pl.when(there)
+            def _():
+                arrive(weight_copies(side, t, me, block))
+                add_from(block, False)
+
+    column = qcol[...].reshape(n * rows, HEAD_DIM)
+    visible = jnp.transpose(column)[0:1, :] <= column[:, 0:1]
+
+    def turn(block, sign):
+        return block * cos[...] + sign * (pltpu.roll(block, HEAD_DIM // 2, 1) * sin[...])
+
+    def dot(a, b, dims):
+        return lax.dot_general(a, b, (dims, ((), ())), preferred_element_type=WIDE)
+
+    def weigh(queries, keys):
+        scores = dot(queries, keys, ((1,), (1,))) * scale
+        masked = jnp.where(visible, scores, -1e30)
+        row_max = jnp.max(masked, axis=-1, keepdims=True)
+        numerators = jnp.where(visible, jnp.exp(masked - row_max), 0.0)
+        return numerators, jnp.sum(numerators, axis=-1, keepdims=True)
+
+    def head_at(kv, h):
+        return pl.ds(pl.multiple_of((kv * group + h) * HEAD_DIM, HEAD_DIM), HEAD_DIM)
+
+    def keys_and_values(qkv, kv):
+        keys = turn(qkv[:, pl.ds(gq + kv * HEAD_DIM, HEAD_DIM)], 1.0).astype(SLIM)
+        return keys, qkv[:, pl.ds(gq + kvw + kv * HEAD_DIM, HEAD_DIM)].astype(SLIM)
+
+    for side in (0, 1):
+        hop(1, side, 1)
+    for kv in range(kvw // HEAD_DIM):
+        keys, values = keys_and_values(qkv_f, kv)
+
+        @pl.loop(0, group)
+        def _(h):
+            at = head_at(kv, h)
+            numerators, totals = weigh(turn(qkv_f[:, at], 1.0).astype(SLIM), keys)
+            result = dot(numerators.astype(SLIM), values, ((1,), (0,))) / totals
+            mixed[:, :, at] = result.astype(SLIM).reshape(n, rows, HEAD_DIM)
+
+    to_all(mixed_copies, begin)
+
+    def rows_of(block):
+        @pl.loop(0, wide // tile)
+        def _(c):
+            at = pl.ds(pl.multiple_of(c * tile, 128), tile)
+            total = jnp.zeros((rows, tile), WIDE)
+            for j in range(n):
+                total += jnp.dot(
+                    xb[block, :, pl.ds(j * depth, depth)], wh[j, :, at], preferred_element_type=WIDE
+                )
+            qkv_b[pl.ds(pl.multiple_of(block * rows, 8), rows), at] = total
+
+    rows_of(me)
+    for t in range(1, n):
+        for side in (0, 1):
+            if t > 1:
+                hop(1, side, t)
+            block, there = behind(side, t)
+            pl.when(there)(lambda: rows_of(block))
+
+    from_all(small_copies)
+    for kv in range(kvw // HEAD_DIM):
+        keys, values = keys_and_values(qkv_b, kv)
+
+        def head(h, sums):
+            at = head_at(kv, h)
+            queries = turn(qkv_b[:, at], 1.0).astype(SLIM)
+            numerators, totals = weigh(queries, keys)
+            rounded = numerators.astype(SLIM)
+            summed = dot(rounded, values, ((1,), (0,)))
+            summed_grad = mg[:, :, at].reshape(n * rows, HEAD_DIM).astype(WIDE) / totals
+            totals_grad = -jnp.sum(summed_grad * (summed / totals), axis=-1, keepdims=True)
+            narrow_grad = summed_grad.astype(SLIM)
+            numer_grad = dot(narrow_grad, values, ((1,), (1,))) + totals_grad
+            score_grad = (numerators * numer_grad * scale).astype(SLIM)
+            query_grad = dot(score_grad, keys, ((1,), (0,))).astype(SLIM)
+            dqkv[:, at] = turn(query_grad.astype(WIDE), -1.0).astype(SLIM)
+            key_grad, value_grad = sums
+            return (
+                key_grad + dot(score_grad, queries, ((0,), (0,))),
+                value_grad + dot(rounded, narrow_grad, ((0,), (0,))),
+            )
+
+        nothing = jnp.zeros(keys.shape, WIDE)
+        key_grad, value_grad = lax.fori_loop(0, group, head, (nothing, nothing))
+        dqkv[:, pl.ds(gq + kv * HEAD_DIM, HEAD_DIM)] = turn(
+            key_grad.astype(SLIM).astype(WIDE), -1.0
+        ).astype(SLIM)
+        dqkv[:, pl.ds(gq + kvw + kv * HEAD_DIM, HEAD_DIM)] = value_grad.astype(SLIM)
+
+    def sum_copy(side, r, block, target):
+        return remote(
+            part.at[block], inbox.at[side, r - 1], bsend.at[side, r], brecv.at[side, r - 1], (section, target)
+        )
+
+    def partial_grad(block, sides_in, r):
+        mine_rows = dqkv[pl.ds(pl.multiple_of(block * rows, 16), rows), :]
+        for j in range(n):
+            part[block, :, pl.ds(j * depth, depth)] = lax.dot_general(
+                mine_rows, wh[j], (((1,), (1,)), ((), ())), preferred_element_type=WIDE
+            ).astype(SLIM)
+        for side in sides_in:
+            _, there = behind(side, 1)
+
+            @pl.when(there)
+            def _():
+                sum_copy(side, r + 1, block, me).wait_recv()
+                part[block] = (part[block].astype(WIDE) + inbox[side, r].astype(WIDE)).astype(SLIM)
+
+    def sum_step(r):
+        for side in (0, 1):
+            block, there = peer(side, r)
+            target, _ = peer(side, 1)
+
+            @pl.when(there)
+            def _():
+                partial_grad(block, (side,), r)
+                sum_copy(side, r, block, target).start()
+
+    sum_step(n - 1)
+    total = tokens[...].astype(WIDE)
+    total += jnp.dot(
+        mixed[me], wo[pl.ds(pl.multiple_of(me * gq, 128), gq), :], preferred_element_type=WIDE
+    )
+    from_all(mixed_copies)
+    for k in range(1, n):
+        source = lax.rem(me + k, n)
+        at = pl.ds(pl.multiple_of(source * gq, 128), gq)
+        total += jnp.dot(mixed_in[source], wo[at, :], preferred_element_type=WIDE)
+    produced[...] = total.astype(SLIM)
+    ahead_copy = remote(produced, ahead, csend.at[0], crecv.at[0], (following, me))
+    ahead_copy.start()
+    for r in range(n - 2, 0, -1):
+        sum_step(r)
+    partial_grad(me, (0, 1), 0)
+
+    widened = saved[...].astype(WIDE)
+    inverse = lax.rsqrt(jnp.mean(widened * widened, axis=-1, keepdims=True) + norm_eps)
+    scaled = part[me].astype(WIDE) * gain[...]
+    inner = jnp.mean(scaled * widened, axis=-1, keepdims=True)
+    project_grad = inverse * scaled - widened * (inverse * inverse * inverse * inner)
+    grads[...] = up[...] + project_grad.astype(SLIM)
+    back_copy = remote(grads, back, csend.at[1], crecv.at[1], (preceding, me))
+    back_copy.start()
+
+    to_all(lambda side, t, target: weight_copies(side, t, target, me), leave)
+    for copies in (small_copies, place_copies, mixed_copies):
+        to_all(copies, leave)
+    for t in range(1, n):
+        for side in (0, 1):
+            block, there = behind(side, t - 1)
+            target, fits = peer(side, 1)
+
+            @pl.when(jnp.logical_and(there, fits))
+            def _():
+                for batch in (0, 1):
+                    leave(row_copies(batch, side, t, block, target))
+
+            block, there = peer(side, t)
+            pl.when(there)(lambda: leave([sum_copy(side, t, block, target)]))
+    ahead_copy.wait()
+    back_copy.wait()
+
+
+def by_heads(n, sections):
+    def step(
+        section_inputs, saved_inputs, output_grads, token_positions, norm_gain,
+        query_weight, keyval_weight, output_weight,
+    ):
+        _, rows, width = section_inputs.shape
+        _, depth, query_width = query_weight.shape
+        gq = query_width // n
+        wide = gq + keyval_weight.shape[2] // n
+
+        def norm(tokens):
+            widened = tokens.astype(WIDE)
+            inverse = lax.rsqrt(jnp.mean(widened * widened, axis=-1, keepdims=True) + norm_eps)
+            return (widened * inverse * norm_gain).astype(SLIM)
+
+        half_dim = HEAD_DIM // 2
+        frequency = rope_base ** (-2.0 * jnp.arange(half_dim, dtype=WIDE) / HEAD_DIM)
+        signs = jnp.ones(half_dim, WIDE)
+        waves = jnp.stack(
+            [jnp.concatenate([frequency, frequency]), jnp.concatenate([-signs, signs])]
+        )
+
+        def shaped(shape, kind=SLIM):
+            return jax.ShapeDtypeStruct(shape, kind)
+
+        def held(*shape, kind=SLIM):
+            return pltpu.VMEM(shape, kind)
+
+        dma = pltpu.SemaphoreType.DMA
+        ahead, back = pl.pallas_call(
+            functools.partial(layer_kernel, n, sections),
+            out_shape=(shaped((rows, width)), shaped((rows, width))),
+            in_specs=[VMEM, VMEM, VMEM, ANY, ANY, ANY, VMEM, VMEM, VMEM, VMEM, VMEM],
+            out_specs=(VMEM,) * 2,
+            scratch_shapes=[
+                held(n, rows, width), held(n, rows, width),
+                held(n, rows, gq), held(n, rows, gq), held(query_width, width), held(n, depth, wide),
+                held(n, 1, rows, kind=jnp.int32), held(n, rows, HEAD_DIM, kind=WIDE),
+                held(n * rows, HEAD_DIM, kind=WIDE), held(n * rows, HEAD_DIM, kind=WIDE),
+                held(n * rows, wide, kind=WIDE), held(n * rows, wide, kind=WIDE),
+                held(n, rows, gq), held(n * rows, wide), held(n, rows, gq),
+                held(n, rows, width), held(2, n, rows, width),
+                held(rows, width), held(rows, width),
+                *[dma((2, n))] * 4, *[dma((2, n, 3))] * 2, *[dma((2, n))] * 8, *[dma((2,))] * 2, dma((4,)),
+            ],
+            compiler_params=pltpu.CompilerParams(
+                collective_id=0, has_side_effects=True, vmem_limit_bytes=60 * 2**20
+            ),
+            name="layer",
+        )(
+            norm(section_inputs[0]), norm(saved_inputs[0]), output_grads[0], output_weight[0],
+            query_weight[0], keyval_weight[0], token_positions[None], waves,
+            section_inputs[0], saved_inputs[0], norm_gain,
+        )
+        return (ahead[None], back[None])
+
+    return step
+
+
 def solution(mesh):
     placed = (
         P("section", "ctx", None),
@@ -159,8 +570,16 @@
         P("section", "ctx", None),
         P("section", None, None),
     )
+    n, sections = mesh.shape["ctx"], mesh.shape["section"]
+
+    def chosen(*blocks):
+        kv_heads = blocks[6].shape[2] // (2 * HEAD_DIM)
+        if n > 1 and sections > 2 and kv_heads % n == 0:
+            return by_heads(n, sections)(*blocks)
+        return shards(*blocks)
+
     return jax.shard_map(
-        shards,
+        chosen,
         mesh=mesh,
         in_specs=placed,
         out_specs=(P("section", "ctx", None), P("section", "ctx", None)),

time: 453 us -> 213 us (0.47)
  Pallas kernels: 0 us -> 199 us
  waiting for transfers between devices: 192 us -> 0 us
  matrix products: 99.9 us -> 0 us
  blocking collectives: 77.1 us -> 0 us
  local copies, waits for them, and re-layouts: 39.6 us -> 3.64 us
  between operations: 14.9 us -> 0.66 us
  other arithmetic: 18.2 us -> 6.09 us
  starting transfers between devices: 6.69 us -> 0 us
    pallas_call x0 -> x1, Pallas kernels: none -> 199 us  [step(): pl.pallas_call(functools.partial(layer_kernel, n, sections), out_shape=(s...]
    all_gather x2 -> x0, waiting for transfers between devices: 168 us -> none  [the longest x1 107 us: shards(): lax.all_gather(query_weight[0], 'ctx', axis=0, tiled=True)]
    dot_general x32 -> x0, matrix products: 84.5 us -> none  [the longest x16 29.8 us: one_head(): jnp.einsum('grs,sd->rgd', rounded, value_block, preferred_element_type=jn...]
    all_gather x4 -> x0, blocking collectives: 73 us -> none  [the longest x1 23.1 us: shards(): lax.all_gather(backward_values, 'ctx', axis=0, tiled=True)]
    dot_general x2 -> x0, local copies, waits for them, and re-layouts: 18.7 us -> none  [the longest x1 12.2 us: project(): jnp.dot(normed, query_matrix, preferred_element_type=jnp.float32)]
    sub x8 -> x0, matrix products: 15.4 us -> none  [one_head(): numerators = jnp.where(visible, jnp.exp(masked - row_max), 0.0)]
    ppermute x2 -> x0, waiting for transfers between devices: 11.6 us -> none  [from_behind(): return lax.ppermute(block, axis, route)]
    reduce_scatter x2 -> x0, waiting for transfers between devices: 11.1 us -> none  [the longest x1 11.1 us: shards(): lax.psum_scatter(value_partial.astype(jnp.bfloat16), 'ctx', scatter_dimen...]
  transfers between devices with their start and end apart: 6 -> 0, of which waited for: 5 -> 0; matrix products, arithmetic and copies ran while one was open for 10% -> 0% of each run, Pallas kernels for 0% -> 0%
where the time goes in v2:
time: 213 us; the launch traced here: 209 us
  Pallas kernels  199 us (93%)
  other arithmetic  6.09 us (3%)
  local copies, waits for them, and re-layouts  3.64 us (2%)
    pallas_call x1, Pallas kernels, step(): pl.pallas_call(functools.partial(layer_kernel, n, sections), out_shape=(s...  199 us

profile of v2, /device:TPU:17, one launch (start us, length us, event | category | flops | bytes accessed | tf_op | source)
XLA Modules:
  0.0 209.2 jit_solution(4652250416059766099)
XLA Ops:
  0.6 1.2 fusion
  1.8 1.2 fusion.3
  3.1 0.1 maximum_bitcast_fusion
  3.2 1.2 pad_maximum_fusion.waves
  4.4 2.4 %fusion.5 = (bf16[112,2048]{1,0:T(8,128)(2,1)}, bf16[112,2048]{1,0:T(8,128)(2,1)}) fusion(f32[112]{0:T(128)S(1)} %get-tuple-element.8, f32[2048]{0:T(1024)} %bitcast.24, bf16[1,112,2048]{2,1,0:T(8,128)(2,1)} %param.9, f32[112]{0:T(128)S(1)} %get-tuple-element.9, bf16[1,112,2048]{2,1,0:T(8,128)(2,1)} %param.8), kind=kLoop, calls=%fused_computation.9 | loop fusion | flops 1835008 | bytes 1844096 | tf_op jit(solution)/shard_map/convert_element_type | solution.py:516
  6.7 198.8 %layer.1 = (bf16[112,2048]{1,0:T(8,128)(2,1)}, bf16[112,2048]{1,0:T(8,128)(2,1)}) custom-call(bf16[112,2048]{1,0:T(8,128)(2,1)} %get-tuple-element.7.nf, bf16[112,2048]{1,0:T(8,128)(2,1)} %get-tuple-element.6.nb, bf16[112,2048]{1,0:T(8,128)(2,1)} %bitcast.23, bf16[2048,2048]{1,0:T(8,128)(2,1)} %bitcast.16, bf16[512,2048]{1,0:T(8,128)(2,1)} %bitcast.19, ...), custom_call_target="tpu_custom_call" | custom-call | tf_op jit(solution)/shard_map/layer/pallas_call | solution.py:532
  205.6 1.8 copy.12
  207.4 1.8 copy.13
  (2 shorter events, 0.0 us)

commit v3 on v2

--- a/solution.py
+++ b/solution.py
@@ -2,6 +2,7 @@
 
 import jax
 import jax.numpy as jnp
+import numpy as np
 from jax import lax
 from jax.experimental import pallas as pl
 from jax.experimental.pallas import tpu as pltpu
@@ -271,6 +272,7 @@
                 pl.when(there)(lambda: arrive(copies(side, t, me)))
 
     send_own(0)
+    send_own(1)
     to_all(place_copies, begin)
     wo_copy = pltpu.make_async_copy(wo_hbm, wo, own.at[0])
     wo_copy.start()
@@ -295,8 +297,9 @@
     for t in range(1, n):
         pl.when(me == t - 1)(lambda: send_weights(0))
         pl.when(n - me == t)(lambda: send_weights(1))
-        for side in (0, 1):
-            hop(0, side, t)
+        for batch in (0, 1):
+            for side in (0, 1):
+                hop(batch, side, t)
 
     wo_copy.wait()
     for j in range(n):
@@ -304,7 +307,6 @@
             up[...], wo[pl.ds(j * gq, gq), :], (((1,), (1,)), ((), ())), preferred_element_type=WIDE
         ).astype(SLIM)
     mg[me] = mgl[me]
-    send_own(1)
     to_all(small_copies, begin)
 
     from_all(place_copies)
@@ -323,10 +325,11 @@
         @pl.loop(0, wide // tile)
         def _(c):
             at = pl.ds(pl.multiple_of(c * tile, 128), tile)
-            term = jnp.dot(
-                xf[:, :, columns].reshape(-1, depth), wh[j, :, at], preferred_element_type=WIDE
-            )
-            qkv_f[:, at] = term if first else qkv_f[:, at] + term
+            for every, total in ((xf, qkv_f), (xb, qkv_b)):
+                term = jnp.dot(
+                    every[:, :, columns].reshape(-1, depth), wh[j, :, at], preferred_element_type=WIDE
+                )
+                total[:, at] = term if first else total[:, at] + term
 
     for copy in mine:
         copy.wait()
@@ -363,8 +366,6 @@
         keys = turn(qkv[:, pl.ds(gq + kv * HEAD_DIM, HEAD_DIM)], 1.0).astype(SLIM)
         return keys, qkv[:, pl.ds(gq + kvw + kv * HEAD_DIM, HEAD_DIM)].astype(SLIM)
 
-    for side in (0, 1):
-        hop(1, side, 1)
     for kv in range(kvw // HEAD_DIM):
         keys, values = keys_and_values(qkv_f, kv)
 
@@ -376,25 +377,6 @@
             mixed[:, :, at] = result.astype(SLIM).reshape(n, rows, HEAD_DIM)
 
     to_all(mixed_copies, begin)
-
-    def rows_of(block):
-        @pl.loop(0, wide // tile)
-        def _(c):
-            at = pl.ds(pl.multiple_of(c * tile, 128), tile)
-            total = jnp.zeros((rows, tile), WIDE)
-            for j in range(n):
-                total += jnp.dot(
-                    xb[block, :, pl.ds(j * depth, depth)], wh[j, :, at], preferred_element_type=WIDE
-                )
-            qkv_b[pl.ds(pl.multiple_of(block * rows, 8), rows), at] = total
-
-    rows_of(me)
-    for t in range(1, n):
-        for side in (0, 1):
-            if t > 1:
-                hop(1, side, t)
-            block, there = behind(side, t)
-            pl.when(there)(lambda: rows_of(block))
 
     from_all(small_copies)
     for kv in range(kvw // HEAD_DIM):
@@ -500,6 +482,18 @@
     back_copy.wait()
 
 
+def norm_kernel(first, second, gain, first_out, second_out):
+    for tokens, normed in ((first, first_out), (second, second_out)):
+        widened = tokens[...].astype(WIDE)
+        inverse = lax.rsqrt(jnp.mean(widened * widened, axis=-1, keepdims=True) + norm_eps)
+        normed[...] = (widened * inverse * gain[...]).astype(SLIM)
+
+
+def hand_kernel(first, second, first_out, second_out):
+    first_out[...] = first[...]
+    second_out[...] = second[...]
+
+
 def by_heads(n, sections):
     def step(
         section_inputs, saved_inputs, output_grads, token_positions, norm_gain,
@@ -510,16 +504,11 @@
         gq = query_width // n
         wide = gq + keyval_weight.shape[2] // n
 
-        def norm(tokens):
-            widened = tokens.astype(WIDE)
-            inverse = lax.rsqrt(jnp.mean(widened * widened, axis=-1, keepdims=True) + norm_eps)
-            return (widened * inverse * norm_gain).astype(SLIM)
-
         half_dim = HEAD_DIM // 2
-        frequency = rope_base ** (-2.0 * jnp.arange(half_dim, dtype=WIDE) / HEAD_DIM)
-        signs = jnp.ones(half_dim, WIDE)
-        waves = jnp.stack(
-            [jnp.concatenate([frequency, frequency]), jnp.concatenate([-signs, signs])]
+        frequency = rope_base ** (-2.0 * np.arange(half_dim) / HEAD_DIM)
+        signs = np.ones(half_dim)
+        waves = jnp.asarray(
+            np.stack([np.concatenate([frequency, frequency]), np.concatenate([-signs, signs])]), WIDE
         )
 
         def shaped(shape, kind=SLIM):
@@ -528,10 +517,14 @@
         def held(*shape, kind=SLIM):
             return pltpu.VMEM(shape, kind)
 
+        pair = (shaped((rows, width)), shaped((rows, width)))
+        normed_f, normed_b = pl.pallas_call(
+            norm_kernel, out_shape=pair, in_specs=[VMEM] * 3, out_specs=(VMEM,) * 2, name="norm"
+        )(section_inputs[0], saved_inputs[0], norm_gain)
         dma = pltpu.SemaphoreType.DMA
         ahead, back = pl.pallas_call(
             functools.partial(layer_kernel, n, sections),
-            out_shape=(shaped((rows, width)), shaped((rows, width))),
+            out_shape=pair,
             in_specs=[VMEM, VMEM, VMEM, ANY, ANY, ANY, VMEM, VMEM, VMEM, VMEM, VMEM],
             out_specs=(VMEM,) * 2,
             scratch_shapes=[
@@ -550,10 +543,13 @@
             ),
             name="layer",
         )(
-            norm(section_inputs[0]), norm(saved_inputs[0]), output_grads[0], output_weight[0],
+            normed_f, normed_b, output_grads[0], output_weight[0],
             query_weight[0], keyval_weight[0], token_positions[None], waves,
             section_inputs[0], saved_inputs[0], norm_gain,
         )
+        ahead, back = pl.pallas_call(
+            hand_kernel, out_shape=pair, in_specs=[VMEM] * 2, out_specs=(VMEM,) * 2, name="hand"
+        )(ahead, back)
         return (ahead[None], back[None])
 
     return step

time: 213 us -> 195 us (0.915)
  Pallas kernels: 199 us -> 191 us
  other arithmetic: 6.09 us -> 0 us
  local copies, waits for them, and re-layouts: 3.64 us -> 0 us
    pallas_call x1 -> x3, Pallas kernels: 199 us -> 191 us  [the longest x1 186 us: step(): pl.pallas_call(functools.partial(layer_kernel, n, sections), out_shape=pa...]
    unnamed x2 -> x0, local copies, waits for them, and re-layouts: 3.64 us -> none
    reduce_sum x2 -> x0, other arithmetic: 2.42 us -> none  [norm(): jnp.mean(widened * widened, axis=-1, keepdims=True) + norm_eps]
    convert_element_type x1 -> x0, other arithmetic: 2.36 us -> none  [norm(): return (widened * inverse * norm_gain).astype(SLIM)]
where the time goes in v3:
time: 195 us; the launch traced here: 191 us
  Pallas kernels  191 us (98%)
    pallas_call x1, Pallas kernels, step(): pl.pallas_call(functools.partial(layer_kernel, n, sections), out_shape=pa...  186 us

profile of v3, /device:TPU:17, one launch (start us, length us, event | category | flops | bytes accessed | tf_op | source)
XLA Modules:
  0.0 191.3 jit_solution(16477860874310066967)
XLA Ops:
  0.6 2.4 %norm.1 = (bf16[112,2048]{1,0:T(8,128)(2,1)}, bf16[112,2048]{1,0:T(8,128)(2,1)}) custom-call(bf16[112,2048]{1,0:T(8,128)(2,1)} %bitcast.11, bf16[112,2048]{1,0:T(8,128)(2,1)} %bitcast.13, f32[1,2048]{1,0:T(1,128)} %gain.3), custom_call_target="tpu_custom_call" | custom-call | tf_op jit(solution)/shard_map/norm/pallas_call | solution.py:521
  3.0 186.2 %layer.1 = (bf16[112,2048]{1,0:T(8,128)(2,1)}, bf16[112,2048]{1,0:T(8,128)(2,1)}) custom-call(bf16[112,2048]{1,0:T(8,128)(2,1)} %get-tuple-element.8.nf, bf16[112,2048]{1,0:T(8,128)(2,1)} %get-tuple-element.9.nb, bf16[112,2048]{1,0:T(8,128)(2,1)} %bitcast.16, bf16[2048,2048]{1,0:T(8,128)(2,1)} %bitcast.9, bf16[512,2048]{1,0:T(8,128)(2,1)} %bitcast.10, ...), custom_call_target="tpu_custom_call" | custom-call | tf_op jit(solution)/shard_map/layer/pallas_call | solution.py:525
  189.2 2.1 %hand.1 = (bf16[112,2048]{1,0:T(8,128)(2,1)}, bf16[112,2048]{1,0:T(8,128)(2,1)}) custom-call(bf16[112,2048]{1,0:T(8,128)(2,1)} %get-tuple-element.10.first, bf16[112,2048]{1,0:T(8,128)(2,1)} %get-tuple-element.11.second), custom_call_target="tpu_custom_call" | custom-call | tf_op jit(solution)/shard_map/hand/pallas_call | solution.py:550
